TPU v7x, 8 devices: a whole 2x2x1 slice. The times are simulated.
8 devices in a mesh: dp: 2 (over y, z), tp: 4 (over x, core).
Axes of the slice: x: 2, y: 2, z: 1, core: 2. Of those that a mesh axis runs over, the one named last changes fastest.
Arguments:
- x: bfloat16 [4096, 2048], P('dp'), parts along dimension 0
- dy: bfloat16 [4096, 2048], P('dp'), parts along dimension 0
- gate: bfloat16 [4096, 5120], P('dp', 'tp'), parts along dimension 0
- up: bfloat16 [4096, 5120], P('dp', 'tp'), parts along dimension 0
- w_gate: bfloat16 [2048, 5120], P(None, 'tp')
- w_up: bfloat16 [2048, 5120], P(None, 'tp')
- w_down: bfloat16 [5120, 2048], P('tp')
Outputs:
- output 1: bfloat16 [4096, 2048], P('dp'), parts along dimension 0
- output 2: bfloat16 [4096, 5120], P('dp', 'tp'), parts along dimension 0
- output 3: bfloat16 [4096, 5120], P('dp', 'tp'), parts along dimension 0
- output 4: bfloat16 [10240, 2048], P(('dp', 'tp')), parts along dimension 0
There are 2 independent parts. A program takes and returns all parts, laid end to end along the dimension named above; an argument that names none is the same for every part.
All inputs are finite; a program needn't handle non-finite values.
Results may differ from a plain program's by a relative error of at most 0.012.
Values are sent between devices in bfloat16 or wider.
A program may use at most 2 GiB of HBM per device.

v0:
```python
import functools

import jax
import jax.numpy as jnp
from jax import lax
from jax.experimental import pallas as pl
from jax.experimental.pallas import tpu as pltpu
from jax.sharding import PartitionSpec as P

MESH = pl.DeviceIdType.MESH
NT = (((1,), (1,)), ((), ()))
TN = (((0,), (0,)), ((), ()))
BF16, F32 = jnp.bfloat16, jnp.float32

CHUNK = 256
HALF = CHUNK // 2
TILE = 256
LATE = 3
C0 = 0.7978845608028654
C1 = 0.044715


def dot(a, b, dims):
    return lax.dot_general(a, b, dims, preferred_element_type=F32)


def kernel(
    x, dy, gate, up, w_gate, w_up, w_down,
    dx, dw_gate, dw_up, dw_down,
    dy_v, gate_v, up_v, hid_v, got_x, got_c, keep, give, x_v,
    w_sem, in_sem, x_sem, give_sem, got_c_sem, send_x_sem, got_x_sem, fin_sem, got_fin_sem,
):
    rows, d = dx.shape
    ff = dw_gate.shape[1]
    n = rows // CHUNK
    pieces = 2 * n
    cols = d // 2
    me = lax.axis_index("tp")
    core = lax.rem(me, 2)
    mate = me + 1 - 2 * core
    across = lax.rem(me + 2, 4)

    def load(src, dst, sem):
        return pltpu.make_async_copy(src, dst, sem)

    def chunk_loads(c):
        r = pl.ds(pl.multiple_of(c * CHUNK, CHUNK), CHUNK)
        return [
            load(dy.at[r], dy_v.at[r], in_sem.at[0, c]),
            load(gate.at[r], gate_v.at[r], in_sem.at[1, c]),
            load(up.at[r], up_v.at[r], in_sem.at[2, c]),
        ]

    def weight_loads(h):
        r = pl.ds(h * cols, cols)
        return [
            load(w_gate.at[r], dw_gate.at[r], w_sem.at[1 + 2 * h]),
            load(w_up.at[r], dw_up.at[r], w_sem.at[2 + 2 * h]),
        ]

    def x_load(k):
        c = pl.ds(pl.multiple_of(k * TILE, TILE), TILE)
        slot = lax.rem(k, 2)
        return load(x.at[:, c], x_v.at[slot], x_sem.at[slot])

    def to(device):
        return dict(device_id={"tp": device}, device_id_type=MESH)

    def own_rows(c):
        return pl.ds(pl.multiple_of(c * CHUNK + core * HALF, HALF), HALF)

    def piece_of(p):
        c, h = p // 2, lax.rem(p, 2)
        return own_rows(c), pl.ds(pl.multiple_of(h * cols, cols), cols)

    def give_copy(p):
        h = lax.rem(p, 2)
        return pltpu.make_async_remote_copy(
            give.at[h], got_c.at[p], give_sem.at[p], got_c_sem.at[p], **to(mate)
        )

    def cross_copy(p):
        r, c = piece_of(p)
        return pltpu.make_async_remote_copy(
            dx.at[r, c], got_x.at[p], send_x_sem.at[p], got_x_sem.at[p], **to(across)
        )

    def final_copy(p):
        r, c = piece_of(p)
        return pltpu.make_async_remote_copy(
            dx.at[r, c], dx.at[r, c], fin_sem.at[p], got_fin_sem.at[p], **to(mate)
        )

    def add_mate(p, h):
        give_copy(p).wait_recv()
        r, c = piece_of(p)
        dx[r, c] = (keep[h] + got_c[p].astype(F32)).astype(BF16)
        cross_copy(p).start()

    def finish(p):
        cross_copy(p).wait()
        r, c = piece_of(p)
        dx[r, c] = (dx[r, c].astype(F32) + got_x[p].astype(F32)).astype(BF16)
        final_copy(p).start()

    first = chunk_loads(0)
    down = load(w_down, dw_down, w_sem.at[0])
    first[0].start()
    down.start()
    first[1].start()
    first[2].start()
    for h in range(2):
        for w in weight_loads(h):
            w.start()

    barrier = pltpu.get_barrier_semaphore()
    for device in (mate, across):
        pl.semaphore_signal(barrier, inc=1, **to(device))
    pl.semaphore_wait(barrier, 2)

    down.wait()

    @pl.loop(0, n)
    def _(c):
        for w in chunk_loads(c):
            w.wait()

        @pl.when(c + 1 < n)
        def _():
            for w in chunk_loads(c + 1):
                w.start()

        r = pl.ds(pl.multiple_of(c * CHUNK, CHUNK), CHUNK)
        for t in range(ff // TILE):
            f = pl.ds(t * TILE, TILE)
            dh = dot(dy_v[r, :], dw_down[f, :], NT)
            g = gate_v[r, f].astype(F32)
            u = up_v[r, f].astype(F32)
            g2 = g * g
            s = 0.5 + 0.5 * jnp.tanh(g * (C0 + (C0 * C1) * g2))
            gelu = g * s
            slope = s + g * (2.0 * C0 + (6.0 * C0 * C1) * g2) * (s - s * s)
            hid_v[r, f] = (gelu * u).astype(BF16)
            gate_v[r, f] = (dh * u * slope).astype(BF16)
            up_v[r, f] = (dh * gelu).astype(BF16)

        @pl.when(c > 0)
        def _():
            add_mate(2 * c - 1, 1)

        mine = own_rows(c)
        other = pl.ds(pl.multiple_of(c * CHUNK + (1 - core) * HALF, HALF), HALF)
        for h in range(2):
            p = 2 * c + h

            @pl.when(c == 0)
            def _():
                for w in weight_loads(h):
                    w.wait()

            @pl.when(c > 0)
            def _():
                give_copy(p - 2).wait_send()

            lhs = jnp.concatenate(
                [
                    jnp.concatenate([gate_v[mine, :], up_v[mine, :]], axis=1),
                    jnp.concatenate([gate_v[other, :], up_v[other, :]], axis=1),
                ],
                axis=0,
            )
            for t in range(cols // TILE):
                w = pl.ds(h * cols + t * TILE, TILE)
                rhs = jnp.concatenate([dw_gate[w, :], dw_up[w, :]], axis=1)
                term = dot(lhs, rhs, NT)
                keep[h, :, t * TILE : (t + 1) * TILE] = term[:HALF]
                give[h, :, t * TILE : (t + 1) * TILE] = term[HALF:].astype(BF16)
            give_copy(p).start()
            if h == 1:
                add_mate(2 * c, 0)

        @pl.when(c == n - 2)
        def _():
            x_load(0).start()

        @pl.when(c >= LATE)
        def _():
            finish(c - LATE)

    add_mate(pieces - 1, 1)
    for p in (pieces - 2, pieces - 1):
        give_copy(p).wait_send()
    done = n - LATE

    tiles = d // TILE

    @pl.loop(0, tiles)
    def _(k):
        x_load(k).wait()

        @pl.when(k + 1 < tiles)
        def _():
            x_load(k + 1).start()

        r = pl.ds(pl.multiple_of(k * TILE, TILE), TILE)
        slot = lax.rem(k, 2)
        dw_gate[r, :] = dot(x_v[slot], gate_v[...], TN).astype(BF16)
        dw_up[r, :] = dot(x_v[slot], up_v[...], TN).astype(BF16)

        @pl.when(lax.rem(k, 2) == 1)
        def _():
            finish(done + k // 2)

    done += tiles // 2

    @pl.loop(0, ff // TILE)
    def _(k):
        f = pl.ds(pl.multiple_of(k * TILE, TILE), TILE)
        for h in range(2):
            c = pl.ds(h * cols, cols)
            dw_down[f, c] = dot(hid_v[:, f], dy_v[:, c], TN).astype(BF16)

        @pl.when(lax.rem(k, 2) == 1)
        def _():
            finish(done + k // 2)

    done += ff // TILE // 2

    @pl.loop(done, pieces)
    def _(p):
        finish(p)

    @pl.loop(0, pieces)
    def _(p):
        final_copy(p).wait()


def store(*refs):
    n = len(refs) // 2
    copies = [pltpu.make_async_copy(refs[i], refs[n + i], refs[-1].at[i]) for i in range(n)]
    for c in copies:
        c.start()
    for c in copies:
        c.wait()


def backward(x, dy, gate, up, w_gate, w_up, w_down):
    rows, d = x.shape
    ff = gate.shape[1]
    pieces = 2 * rows // CHUNK
    cols = d // 2
    hbm = pl.BlockSpec(memory_space=pl.ANY)
    sem = pltpu.SemaphoreType.DMA
    parts = pl.pallas_call(
        kernel,
        out_shape=tuple(pltpu.VMEM(s, BF16) for s in ((rows, d), (d, ff), (d, ff), (ff, d))),
        in_specs=[hbm] * 7,
        out_specs=(pl.BlockSpec(memory_space=pltpu.VMEM),) * 4,
        scratch_shapes=[
            pltpu.VMEM((rows, d), BF16),
            pltpu.VMEM((rows, ff), BF16),
            pltpu.VMEM((rows, ff), BF16),
            pltpu.VMEM((rows, ff), BF16),
            pltpu.VMEM((pieces, HALF, cols), BF16),
            pltpu.VMEM((pieces, HALF, cols), BF16),
            pltpu.VMEM((2, HALF, cols), F32),
            pltpu.VMEM((2, HALF, cols), BF16),
            pltpu.VMEM((2, rows, TILE), BF16),
            sem((5,)),
            sem((3, rows // CHUNK)),
            sem((2,)),
        ]
        + [sem((pieces,))] * 6,
        compiler_params=pltpu.CompilerParams(
            collective_id=0, has_side_effects=True, vmem_limit_bytes=39 * 2**20
        ),
        cost_estimate=pl.CostEstimate(
            flops=12 * rows * d * ff, bytes_accessed=64 * 2**20, transcendentals=rows * ff
        ),
        name="mlp_backward",
    )(x, dy, gate, up, w_gate, w_up, w_down)
    return pl.pallas_call(
        store,
        out_shape=tuple(pltpu.HBM(p.shape, p.dtype) for p in parts),
        in_specs=[pl.BlockSpec(memory_space=pltpu.VMEM)] * len(parts),
        out_specs=(pl.BlockSpec(memory_space=pltpu.HBM),) * len(parts),
        scratch_shapes=[sem((len(parts),))],
        compiler_params=pltpu.CompilerParams(vmem_limit_bytes=2**20),
        name="store",
    )(*parts)


def solution(mesh):
    tokens, columns, down = P("dp", None), P(None, "tp"), P("tp", None)
    return jax.shard_map(
        backward,
        mesh=mesh,
        in_specs=(tokens, tokens, P("dp", "tp"), P("dp", "tp"), columns, columns, down),
        out_specs=(tokens, P("dp", "tp"), P("dp", "tp"), P(("dp", "tp"), None)),
        check_vma=False,
    )
```

profile of v0, /device:TPU:0, one launch (start us, length us, event | category | flops | bytes accessed | tf_op | source)
XLA Modules:
  0.0 116.1 jit_solution(5590021897775151068)
XLA Ops:
  0.6 107.1 %mlp_backward.1 = (bf16[2048,2048]{1,0:T(8,128)(2,1)S(1)}, bf16[2048,1280]{1,0:T(8,128)(2,1)S(1)}, bf16[2048,1280]{1,0:T(8,128)(2,1)S(1)}, bf16[1280,2048]{1,0:T(8,128)(2,1)S(1)}) custom-call(bf16[2048,2048]{1,0:T(8,128)(2,1)} %x.1, bf16[2048,2048]{1,0:T(8,128)(2,1)} %dy.1, bf16[2048,1280]{1,0:T(8,128)(2,1)} %gate.1, bf16[2048,1280]{1,0:T(8,128)(2,1)} %up.1, ...), custom_call_target="tpu_custom_call" | custom-call | flops 64424509440 | bytes 67108864 | tf_op jit(solution)/shard_map/mlp_backward/pallas_call | solution.py:254
  107.8 8.3 %store.1 = (bf16[2048,2048]{1,0:T(8,128)(2,1)}, bf16[2048,1280]{1,0:T(8,128)(2,1)}, bf16[2048,1280]{1,0:T(8,128)(2,1)}, bf16[1280,2048]{1,0:T(8,128)(2,1)}) custom-call(bf16[2048,2048]{1,0:T(8,128)(2,1)S(1)} %get-tuple-element.8.refs_0_, bf16[2048,1280]{1,0:T(8,128)(2,1)S(1)} %get-tuple-element.9.refs_1_, bf16[2048,1280]{1,0:T(8,128)(2,1)S(1)} %get-tuple-element.10.refs_2_, ...), custom_call_target="tpu_custom_call" | custom-call | tf_op jit(solution)/shard_map/store/pallas_call | solution.py:282
where the time goes:
time: 116 us
  Pallas kernels  115 us (99%)
    pallas_call x1, Pallas kernels, backward(): pl.pallas_call(kernel, out_shape=tuple((pltpu.VMEM(s, BF16) for s in ((ro...  107 us
    pallas_call x1, Pallas kernels, backward(): pl.pallas_call(store, out_shape=tuple((pltpu.HBM(p.shape, p.dtype) for p...  8.31 us

commit v1 on v0

v1 whole, which is shorter than its diff:
```python
import functools

import jax
import jax.numpy as jnp
from jax import lax
from jax.experimental import pallas as pl
from jax.experimental.pallas import tpu as pltpu
from jax.sharding import PartitionSpec as P

MESH = pl.DeviceIdType.MESH
NT = (((1,), (1,)), ((), ()))
TN = (((0,), (0,)), ((), ()))
BF16, F32 = jnp.bfloat16, jnp.float32

CHUNK = 256
HALF = CHUNK // 2
TILE = 256
PIECE = 512
RING = 8
SPLIT = 4
C0 = 0.7978845608028654
C1 = 0.044715


def dot(a, b, dims):
    return lax.dot_general(a, b, dims, preferred_element_type=F32)


def kernel(
    x, dy, gate, up, w_gate, w_up, w_down,
    dx, dw_gate, dw_up, dw_down,
    dy_v, gate_v, up_v, hid_v, got_x, got_c, keep, give, x_v,
    w_sem, in_sem, x_sem, give_sem, got_c_sem, send_x_sem, got_x_sem, fin_sem, got_fin_sem,
):
    rows, d = dx.shape
    ff = dw_gate.shape[1]
    n = rows // CHUNK
    per = d // PIECE
    pieces = per * n
    downs = [(0, 2), (2, 5)]
    last = n - 1
    me = lax.axis_index("tp")
    core = lax.rem(me, 2)
    mate = me + 1 - 2 * core
    across = lax.rem(me + 2, 4)

    def load(src, dst, sem):
        return pltpu.make_async_copy(src, dst, sem)

    def chunk_loads(c):
        r = pl.ds(pl.multiple_of(c * CHUNK, CHUNK), CHUNK)
        return [
            load(dy.at[r], dy_v.at[r], in_sem.at[0, lax.rem(c, 2)]),
            load(gate.at[r], gate_v.at[r], in_sem.at[1, lax.rem(c, 2)]),
            load(up.at[r], up_v.at[r], in_sem.at[2, lax.rem(c, 2)]),
        ]

    def weight_loads(j):
        r = pl.ds(j * PIECE, PIECE)
        return [
            load(w_gate.at[r], dw_gate.at[r], w_sem.at[0, j]),
            load(w_up.at[r], dw_up.at[r], w_sem.at[1, j]),
        ]

    def down_load(b):
        lo, hi = downs[b]
        r = pl.ds(lo * TILE, (hi - lo) * TILE)
        return load(w_down.at[r], dw_down.at[r], w_sem.at[2, b])

    def x_load(k):
        c = pl.ds(pl.multiple_of(k * TILE, TILE), TILE)
        slot = lax.rem(k, 2)
        return load(x.at[:, c], x_v.at[slot], x_sem.at[slot])

    def to(device):
        return dict(device_id={"tp": device}, device_id_type=MESH)

    def own_rows(c):
        return pl.ds(pl.multiple_of(c * CHUNK + core * HALF, HALF), HALF)

    def piece_of(p):
        c, j = p // per, lax.rem(p, per)
        return own_rows(c), pl.ds(pl.multiple_of(j * PIECE, PIECE), PIECE)

    def give_copy(p):
        return pltpu.make_async_remote_copy(
            give.at[lax.rem(p, per)],
            got_c.at[p],
            give_sem.at[lax.rem(p, per)],
            got_c_sem.at[lax.rem(p, RING)],
            **to(mate),
        )

    def cross(refs, slot):
        return pltpu.make_async_remote_copy(
            got_c.at[refs], got_x.at[refs], send_x_sem, got_x_sem.at[slot], **to(across)
        )

    def final_copy(r, c):
        return pltpu.make_async_remote_copy(
            dx.at[r, c], dx.at[r, c], fin_sem, got_fin_sem, **to(mate)
        )

    def add_mate(p):
        give_copy(p).wait_recv()
        got_c[p] = (keep[lax.rem(p, per)] + got_c[p].astype(F32)).astype(BF16)
        slot = jnp.where(p < last * per, p // per, p - last * (per - 1))
        cross(pl.ds(p, 1), slot).start()

    def whole_sum(p):
        r, c = piece_of(p)
        dx[r, c] = (got_c[p].astype(F32) + got_x[p].astype(F32)).astype(BF16)

    def finish_chunk(c):
        cross(pl.ds(pl.multiple_of(c * per, per), per), c).wait_recv()
        for j in range(per):
            whole_sum(c * per + j)
        final_copy(own_rows(c), pl.ds(0, d)).start()

    def finish_last(j):
        p = last * per + j
        cross(pl.ds(p, 1), last + j).wait_recv()
        whole_sum(p)
        final_copy(*piece_of(p)).start()

    def hidden(r, lo, hi):
        for t in range(lo, hi):
            f = pl.ds(t * TILE, TILE)
            dh = dot(dy_v[r, :], dw_down[f, :], NT)
            g = gate_v[r, f].astype(F32)
            u = up_v[r, f].astype(F32)
            g2 = g * g
            s = 0.5 + 0.5 * jnp.tanh(g * (C0 + (C0 * C1) * g2))
            gelu = g * s
            slope = s + g * (2.0 * C0 + (6.0 * C0 * C1) * g2) * (s - s * s)
            hid_v[r, f] = (gelu * u).astype(BF16)
            gate_v[r, f] = (dh * u * slope).astype(BF16)
            up_v[r, f] = (dh * gelu).astype(BF16)

    first = chunk_loads(0)
    first[0].start()
    down_load(0).start()
    first[1].start()
    first[2].start()
    for b in range(1, len(downs)):
        down_load(b).start()

    barrier = pltpu.get_barrier_semaphore()
    for device in (mate, across):
        pl.semaphore_signal(barrier, inc=1, **to(device))

    @pl.loop(0, n)
    def _(c):
        for w in chunk_loads(c):
            w.wait()

        r = pl.ds(pl.multiple_of(c * CHUNK, CHUNK), CHUNK)

        @pl.when(c == 0)
        def _():
            for b, (lo, hi) in enumerate(downs):
                down_load(b).wait()
                for j in range(per * b // len(downs), per * (b + 1) // len(downs)):
                    for w in weight_loads(j):
                        w.start()
                hidden(r, lo, hi)
            pl.semaphore_wait(barrier, 2)

        @pl.when(c > 0)
        def _():
            hidden(r, 0, ff // TILE)

        @pl.when(c + 1 < n)
        def _():
            for w in chunk_loads(c + 1):
                w.start()

        @pl.when(c > 1)
        def _():
            add_mate(per * c - 2)

        @pl.when(c > 0)
        def _():
            add_mate(per * c - 1)

        mine = own_rows(c)
        other = pl.ds(pl.multiple_of(c * CHUNK + (1 - core) * HALF, HALF), HALF)
        for j in range(per):
            p = per * c + j

            @pl.when(c == 0)
            def _():
                for w in weight_loads(j):
                    w.wait()

            @pl.when(c > 0)
            def _():
                give_copy(p - per).wait_send()

            lhs = jnp.concatenate(
                [
                    jnp.concatenate([gate_v[mine, :], up_v[mine, :]], axis=1),
                    jnp.concatenate([gate_v[other, :], up_v[other, :]], axis=1),
                ],
                axis=0,
            )
            for t in range(PIECE // TILE):
                w = pl.ds(j * PIECE + t * TILE, TILE)
                rhs = jnp.concatenate([dw_gate[w, :], dw_up[w, :]], axis=1)
                term = dot(lhs, rhs, NT)
                keep[j, :, t * TILE : (t + 1) * TILE] = term[:HALF]
                give[j, :, t * TILE : (t + 1) * TILE] = term[HALF:].astype(BF16)
            give_copy(p).start()

            if j > 0:

                @pl.when(c == 0)
                def _():
                    add_mate(p - 1)

            if j > 1:

                @pl.when(c > 0)
                def _():
                    add_mate(p - 2)

        @pl.when(c == n - 2)
        def _():
            x_load(0).start()

        @pl.when((c > 2) & (lax.rem(c, 2) == 1))
        def _():
            finish_chunk((c - 3) // 2)

    for p in (pieces - 2, pieces - 1):
        add_mate(p)
    for p in range(pieces - per, pieces):
        give_copy(p).wait_send()
    tiles = d // TILE

    @pl.loop(0, tiles)
    def _(k):
        x_load(k).wait()

        @pl.when(k + 1 < tiles)
        def _():
            x_load(k + 1).start()

        r = pl.ds(pl.multiple_of(k * TILE, TILE), TILE)
        slot = lax.rem(k, 2)
        dw_gate[r, :] = dot(x_v[slot], gate_v[...], TN).astype(BF16)
        dw_up[r, :] = dot(x_v[slot], up_v[...], TN).astype(BF16)
        @pl.when(lax.rem(k, 4) == 1)
        def _():
            finish_chunk(3 + k // 4)

    @pl.loop(0, ff // TILE)
    def _(k):
        f = pl.ds(pl.multiple_of(k * TILE, TILE), TILE)
        for h in range(2):
            c = pl.ds(h * (d // 2), d // 2)
            dw_down[f, c] = dot(hid_v[:, f], dy_v[:, c], TN).astype(BF16)

        @pl.when(k == 1)
        def _():
            finish_chunk(5)

    finish_chunk(6)
    for j in range(per):
        finish_last(j)

    total = pltpu.make_async_remote_copy(got_c, got_x, send_x_sem, got_fin_sem, **to(across))
    total.wait_send()
    total = pltpu.make_async_remote_copy(got_x, got_x, fin_sem, got_fin_sem, **to(mate))
    total.wait()


def store(*refs):
    n = len(refs) // 2
    copies = []
    for i in range(n):
        step = refs[i].shape[0] // SPLIT
        for k in range(SPLIT):
            r = pl.ds(k * step, step)
            copies.append(pltpu.make_async_copy(refs[i].at[r], refs[n + i].at[r], refs[-1].at[i, k]))
    for c in copies:
        c.start()
    for c in copies:
        c.wait()


def backward(x, dy, gate, up, w_gate, w_up, w_down):
    rows, d = x.shape
    ff = gate.shape[1]
    per = d // PIECE
    pieces = per * rows // CHUNK
    hbm = pl.BlockSpec(memory_space=pl.ANY)
    sem = pltpu.SemaphoreType.DMA
    parts = pl.pallas_call(
        kernel,
        out_shape=tuple(pltpu.VMEM(s, BF16) for s in ((rows, d), (d, ff), (d, ff), (ff, d))),
        in_specs=[hbm] * 7,
        out_specs=(pl.BlockSpec(memory_space=pltpu.VMEM),) * 4,
        scratch_shapes=[
            pltpu.VMEM((rows, d), BF16),
            pltpu.VMEM((rows, ff), BF16),
            pltpu.VMEM((rows, ff), BF16),
            pltpu.VMEM((rows, ff), BF16),
            pltpu.VMEM((pieces, HALF, PIECE), BF16),
            pltpu.VMEM((pieces, HALF, PIECE), BF16),
            pltpu.VMEM((per, HALF, PIECE), F32),
            pltpu.VMEM((per, HALF, PIECE), BF16),
            pltpu.VMEM((2, rows, TILE), BF16),
            sem((3, per)),
            sem((3, 2)),
            sem((2,)),
            sem((per,)),
            sem((RING,)),
            sem,
            sem((rows // CHUNK - 1 + per,)),
            sem,
            sem,
        ],
        compiler_params=pltpu.CompilerParams(
            collective_id=0, has_side_effects=True, vmem_limit_bytes=39 * 2**20
        ),
        cost_estimate=pl.CostEstimate(
            flops=12 * rows * d * ff, bytes_accessed=64 * 2**20, transcendentals=rows * ff
        ),
        name="mlp_backward",
    )(x, dy, gate, up, w_gate, w_up, w_down)
    return pl.pallas_call(
        store,
        out_shape=tuple(pltpu.HBM(p.shape, p.dtype) for p in parts),
        in_specs=[pl.BlockSpec(memory_space=pltpu.VMEM)] * len(parts),
        out_specs=(pl.BlockSpec(memory_space=pltpu.HBM),) * len(parts),
        scratch_shapes=[sem((len(parts), SPLIT))],
        compiler_params=pltpu.CompilerParams(vmem_limit_bytes=2**20),
        name="store",
    )(*parts)


def solution(mesh):
    tokens, columns, down = P("dp", None), P(None, "tp"), P("tp", None)
    return jax.shard_map(
        backward,
        mesh=mesh,
        in_specs=(tokens, tokens, P("dp", "tp"), P("dp", "tp"), columns, columns, down),
        out_specs=(tokens, P("dp", "tp"), P("dp", "tp"), P(("dp", "tp"), None)),
        check_vma=False,
    )
```

time: 116 us -> 112 us (0.966)
  Pallas kernels: 115 us -> 111 us
    pallas_call x1, Pallas kernels: 107 us -> 103 us  [backward(): pl.pallas_call(kernel, out_shape=tuple((pltpu.VMEM(s, BF16) for s in ((ro...]
where the time goes in v1:
time: 112 us; the launch traced here: 111 us
  Pallas kernels  111 us (99%)
    pallas_call x1, Pallas kernels, backward(): pl.pallas_call(kernel, out_shape=tuple((pltpu.VMEM(s, BF16) for s in ((ro...  103 us
    pallas_call x1, Pallas kernels, backward(): pl.pallas_call(store, out_shape=tuple((pltpu.HBM(p.shape, p.dtype) for p...  8.17 us

profile of v1, /device:TPU:0, one launch (start us, length us, event | category | flops | bytes accessed | tf_op | source)
XLA Modules:
  0.0 111.5 jit_solution(5496171181722414092)
XLA Ops:
  0.6 102.7 %mlp_backward.1 = (bf16[2048,2048]{1,0:T(8,128)(2,1)S(1)}, bf16[2048,1280]{1,0:T(8,128)(2,1)S(1)}, bf16[2048,1280]{1,0:T(8,128)(2,1)S(1)}, bf16[1280,2048]{1,0:T(8,128)(2,1)S(1)}) custom-call(bf16[2048,2048]{1,0:T(8,128)(2,1)} %x.1, bf16[2048,2048]{1,0:T(8,128)(2,1)} %dy.1, bf16[2048,1280]{1,0:T(8,128)(2,1)} %gate.1, bf16[2048,1280]{1,0:T(8,128)(2,1)} %up.1, ...), custom_call_target="tpu_custom_call" | custom-call | flops 64424509440 | bytes 67108864 | tf_op jit(solution)/shard_map/mlp_backward/pallas_call | solution.py:299
  103.3 8.2 %store.1 = (bf16[2048,2048]{1,0:T(8,128)(2,1)}, bf16[2048,1280]{1,0:T(8,128)(2,1)}, bf16[2048,1280]{1,0:T(8,128)(2,1)}, bf16[1280,2048]{1,0:T(8,128)(2,1)}) custom-call(bf16[2048,2048]{1,0:T(8,128)(2,1)S(1)} %get-tuple-element.8.refs_0_, bf16[2048,1280]{1,0:T(8,128)(2,1)S(1)} %get-tuple-element.9.refs_1_, bf16[2048,1280]{1,0:T(8,128)(2,1)S(1)} %get-tuple-element.10.refs_2_, ...), custom_call_target="tpu_custom_call" | custom-call | tf_op jit(solution)/shard_map/store/pallas_call | solution.py:332

commit v2 on v1

--- a/solution.py
+++ b/solution.py
@@ -16,8 +16,8 @@
 HALF = CHUNK // 2
 TILE = 256
 PIECE = 512
-RING = 8
-SPLIT = 4
+RING = 6
+SPLIT = 2
 C0 = 0.7978845608028654
 C1 = 0.044715
 
@@ -37,7 +37,7 @@
     n = rows // CHUNK
     per = d // PIECE
     pieces = per * n
-    downs = [(0, 2), (2, 5)]
+    downs = [(0, 1), (1, 3), (3, 5)]
     last = n - 1
     me = lax.axis_index("tp")
     core = lax.rem(me, 2)
@@ -132,7 +132,7 @@
             g2 = g * g
             s = 0.5 + 0.5 * jnp.tanh(g * (C0 + (C0 * C1) * g2))
             gelu = g * s
-            slope = s + g * (2.0 * C0 + (6.0 * C0 * C1) * g2) * (s - s * s)
+            slope = s + (g * (s * (1.0 - s))) * (2.0 * C0 + (6.0 * C0 * C1) * g2)
             hid_v[r, f] = (gelu * u).astype(BF16)
             gate_v[r, f] = (dh * u * slope).astype(BF16)
             up_v[r, f] = (dh * gelu).astype(BF16)
@@ -143,7 +143,7 @@
     first[1].start()
     first[2].start()
     for b in range(1, len(downs)):
-        down_load(b).start()
+        down_load(b).start(priority=1)
 
     barrier = pltpu.get_barrier_semaphore()
     for device in (mate, across):

time: 112 us -> 111 us (level)
  no operation moved by 1% of the time
where the time goes in v2:
time: 111 us
  Pallas kernels  110 us (99%)
    pallas_call x1, Pallas kernels, backward(): pl.pallas_call(kernel, out_shape=tuple((pltpu.VMEM(s, BF16) for s in ((ro...  102 us
    pallas_call x1, Pallas kernels, backward(): pl.pallas_call(store, out_shape=tuple((pltpu.HBM(p.shape, p.dtype) for p...  8.15 us

profile of v2, /device:TPU:0, one launch (start us, length us, event | category | flops | bytes accessed | tf_op | source)
XLA Modules:
  0.0 111.1 jit_solution(15272559638806842390)
XLA Ops:
  0.6 102.3 %mlp_backward.1 = (bf16[2048,2048]{1,0:T(8,128)(2,1)S(1)}, bf16[2048,1280]{1,0:T(8,128)(2,1)S(1)}, bf16[2048,1280]{1,0:T(8,128)(2,1)S(1)}, bf16[1280,2048]{1,0:T(8,128)(2,1)S(1)}) custom-call(bf16[2048,2048]{1,0:T(8,128)(2,1)} %x.1, bf16[2048,2048]{1,0:T(8,128)(2,1)} %dy.1, bf16[2048,1280]{1,0:T(8,128)(2,1)} %gate.1, bf16[2048,1280]{1,0:T(8,128)(2,1)} %up.1, ...), custom_call_target="tpu_custom_call" | custom-call | flops 64424509440 | bytes 67108864 | tf_op jit(solution)/shard_map/mlp_backward/pallas_call | solution.py:299
  103.0 8.1 %store.1 = (bf16[2048,2048]{1,0:T(8,128)(2,1)}, bf16[2048,1280]{1,0:T(8,128)(2,1)}, bf16[2048,1280]{1,0:T(8,128)(2,1)}, bf16[1280,2048]{1,0:T(8,128)(2,1)}) custom-call(bf16[2048,2048]{1,0:T(8,128)(2,1)S(1)} %get-tuple-element.8.refs_0_, bf16[2048,1280]{1,0:T(8,128)(2,1)S(1)} %get-tuple-element.9.refs_1_, bf16[2048,1280]{1,0:T(8,128)(2,1)S(1)} %get-tuple-element.10.refs_2_, ...), custom_call_target="tpu_custom_call" | custom-call | tf_op jit(solution)/shard_map/store/pallas_call | solution.py:332
